TPU v7x, 32 devices: a whole 2x2x4 slice. The times are simulated.
32 devices in a mesh: gx: 4 (over y, core), gy: 4 (over z), gz: 2 (over x).
Axes of the slice: x: 2, y: 2, z: 4, core: 2. Of those that a mesh axis runs over, the one named last changes fastest.
Arguments:
- order_param: float32 [16, 64, 256], P('gx', 'gy', 'gz'), may hold values from -1 to 1
- density: float32 [16, 64, 256], P('gx', 'gy', 'gz'), may hold values from 0.7 to 1.3
- velocity: float32 [3, 16, 64, 256], P(None, 'gx', 'gy', 'gz'), may hold values from -0.3 to 0.3
Outputs:
- final_order: float32 [16, 64, 256], P('gx', 'gy', 'gz')
- populations: float32 [19, 16, 64, 256], P(None, 'gx', 'gy', 'gz')
All inputs are finite; a program needn't handle non-finite values.
Results may differ from a plain program's by a relative error of at most 0.0001.
Values sent between devices are 32-bit elements; how exact they have to be, the bound alone decides.
A program may use at most 64 MiB of HBM per device.

v0:
```python
import functools

import jax
import jax.numpy as jnp
from jax import lax
from jax.experimental import pallas as pl
from jax.experimental.pallas import tpu as pltpu
from jax.sharding import PartitionSpec as P

ITERS = 5
MESH = pl.DeviceIdType.MESH
DIRS = [
    (0, 0, 0),
    (1, 0, 0),
    (-1, 0, 0),
    (0, 1, 0),
    (0, -1, 0),
    (0, 0, 1),
    (0, 0, -1),
    (1, 1, 0),
    (-1, -1, 0),
    (1, -1, 0),
    (-1, 1, 0),
    (1, 0, 1),
    (-1, 0, -1),
    (1, 0, -1),
    (-1, 0, 1),
    (0, 1, 1),
    (0, -1, -1),
    (0, 1, -1),
    (0, -1, 1),
]
WEIGHTS = [1.0 / 3.0] + [1.0 / 18.0] * 6 + [1.0 / 36.0] * 12
quadratic = -0.1
quartic = 0.1
stiffness = 0.02
mobility = 0.5
relax_time = 0.8

SIGNS = (1, -1)
INDEX = {1: 0, -1: 1}
CROSS = [{s: [i for i in range(19) if DIRS[i][d] == s] for s in SIGNS} for d in range(3)]
EDGES = [(a, b) for a in SIGNS for b in SIGNS]
LANES = 8


def neighbours():
    out = []
    for d in range(3):
        for s in SIGNS:
            out.append(tuple(s if k == d else 0 for k in range(3)))
    out += [(a, b, 0) for a, b in EDGES]
    out += [(a, 0, b) for a, b in EDGES]
    out += [(0, a, b) for a, b in EDGES]
    return out


def kernel(sizes, order_in, dens_in, vel_in, order, pops, post, *scratch):
    (ax, ay, az, rax, ray, raz, raxy, raxz, rayz) = scratch[0:9]
    (by, bz, rbx, rby, rbz, rbxy, rbxz, rbyzr, rbyzc) = scratch[9:18]
    (cx_, cy_, cz_, rcx, rcy, rcz) = scratch[18:24]
    (sa, ra, sb, rb, sc, rc) = scratch[24:30]
    X, Y, Z = order.shape
    me = [lax.axis_index(a) for a in ("gx", "gy", "gz")]

    def device(off):
        return {
            a: lax.rem(me[k] + (off[k] + sizes[k]), sizes[k]) if off[k] else me[k]
            for k, a in enumerate(("gx", "gy", "gz"))
        }

    barrier = pltpu.get_barrier_semaphore()
    for off in neighbours():
        pl.semaphore_signal(barrier, inc=1, device_id=device(off), device_id_type=MESH)

    lane = lax.broadcasted_iota(jnp.int32, (Y, Z), 1)
    row = lax.broadcasted_iota(jnp.int32, (Y, Z), 0)
    lane8 = lax.broadcasted_iota(jnp.int32, (8, Z), 1)
    row8 = lax.broadcasted_iota(jnp.int32, (8, Z), 0)
    lane1 = lax.broadcasted_iota(jnp.int32, (1, Z), 1)

    def roll(v, s, axis):
        s = s % v.shape[axis]
        return v if s == 0 else pltpu.roll(v, s, axis)

    def zend(s):
        return 0 if s == 1 else Z - 1

    def yend(s):
        return 0 if s == 1 else Y - 1

    def zshift(v, s, packed, at):
        col = roll(packed, zend(s) - at, 1)
        return jnp.where(lane == zend(s), col, roll(v, s, 1))

    def yshift(v, s, halo):
        return jnp.where(row == yend(s), jnp.broadcast_to(halo, v.shape), roll(v, s, 0))

    def rowshift(v, s, edge, lanes):
        return jnp.where(lanes == zend(s), roll(edge, s, 1), roll(v, s, 1))

    def pack(fields, s):
        acc = jnp.zeros((Y, Z), jnp.float32)
        for slot, planes in enumerate(fields):
            for x in range(X):
                at = slot * LANES + 1 + x
                depth_lane = planes[x][1]
                acc = jnp.where(lane == at, roll(planes[x][0], at - depth_lane, 1), acc)
        return acc

    def run(messages, ssem, rsem):
        copies = []
        for k, (src, dst, off) in enumerate(messages):
            copy = pltpu.make_async_remote_copy(
                src_ref=src,
                dst_ref=dst,
                send_sem=ssem.at[k],
                recv_sem=rsem.at[k],
                device_id=device(off),
                device_id_type=MESH,
            )
            copy.start()
            copies.append(copy)
        return copies

    def finish(copies):
        for copy in copies:
            copy.wait_recv()
        for copy in copies:
            copy.wait_send()

    for ref in (ay, by, cy_):
        ref[...] = jnp.zeros_like(ref)

    for x in range(X):
        order[x] = order_in[x]
        r = dens_in[x]
        u = [vel_in[d, x] for d in range(3)]
        usq = 1.0 - 1.5 * (u[0] * u[0] + u[1] * u[1] + u[2] * u[2])
        for i in range(19):
            along = None
            for d in range(3):
                if DIRS[i][d]:
                    t = u[d] if DIRS[i][d] == 1 else -u[d]
                    along = t if along is None else along + t
            if along is None:
                pops[i, x] = WEIGHTS[i] * r * usq
            else:
                pops[i, x] = WEIGHTS[i] * r * (usq + 3.0 * along + 4.5 * along * along)
    pl.semaphore_wait(barrier, len(neighbours()))

    def moments(ps):
        rho = ps[0]
        for i in range(1, 19):
            rho = rho + ps[i]
        moms = []
        for d in range(3):
            up = functools.reduce(lambda a, b: a + b, [ps[i] for i in CROSS[d][1]])
            down = functools.reduce(lambda a, b: a + b, [ps[i] for i in CROSS[d][-1]])
            moms.append(up - down)
        return rho, moms

    def chemical(o, beside):
        return quadratic * o + quartic * o * o * o - stiffness * (beside - 6.0 * o)

    def step(_, carry):
        O = [order[x] for x in range(X)]
        for s in SIGNS:
            si = INDEX[s]
            for depth in range(2):
                y = Y - 1 - depth if s == 1 else depth
                for x in range(X):
                    by[si, depth, 1 + x : 2 + x, :] = O[x][y : y + 1, :]
            bz[si] = pack(
                [
                    [(O[x], Z - 1 - depth if s == 1 else depth) for x in range(X)]
                    for depth in range(2)
                ],
                s,
            )
        messages = []
        for s in SIGNS:
            si = INDEX[s]
            planes = order.at[pl.ds(X - 2, 2)] if s == 1 else order.at[pl.ds(0, 2)]
            messages.append((planes, rbx.at[si], (s, 0, 0)))
            messages.append((by.at[si], rby.at[si], (0, s, 0)))
            messages.append((bz.at[si], rbz.at[si], (0, 0, s)))
        for e, (a, b) in enumerate(EDGES):
            messages.append((by.at[INDEX[b], 0], rbxy.at[e], (a, b, 0)))
            messages.append((bz.at[INDEX[b]], rbxz.at[e], (a, 0, b)))
            messages.append((by.at[INDEX[a], 0], rbyzr.at[e], (0, a, b)))
            half = bz.at[INDEX[b], pl.ds(Y - 8, 8)] if a == 1 else bz.at[INDEX[b], pl.ds(0, 8)]
            messages.append((half, rbyzc.at[e], (0, a, b)))
        finish(run(messages, sb, rb))

        edge = {ab: e for e, ab in enumerate(EDGES)}
        OX = {-2: rbx[0, 0], -1: rbx[0, 1], X: rbx[1, 0], X + 1: rbx[1, 1]}
        for x in range(X):
            OX[x] = O[x]

        def order_y(x, s):
            return yshift(O[x], s, rby[INDEX[s], 0, 1 + x : 2 + x, :])

        def order_z(x, s):
            return zshift(O[x], s, rbz[INDEX[s]], 1 + x)

        C, pairs = {}, []
        for x in range(X):
            near = {(0, 1): OX[x - 1], (0, -1): OX[x + 1]}
            for s in SIGNS:
                near[(1, s)], near[(2, s)] = order_y(x, s), order_z(x, s)
            C[x] = chemical(O[x], functools.reduce(lambda a, b: a + b, near.values()))
            pairs.append({k: O[x] + v for k, v in near.items()})
        for s in SIGNS:
            x = -1 if s == 1 else X
            far = X - 1 if s == 1 else 0
            p = OX[x]
            beside = OX[x - 1] + OX[x + 1]
            for t in SIGNS:
                e = edge[(s, t)]
                beside = beside + yshift(p, t, rbxy[e, 1 + far : 2 + far, :])
                beside = beside + zshift(p, t, rbxz[e], 1 + far)
            C[x] = chemical(p, beside)
        CY, CZ = {}, {}
        for s in SIGNS:
            near = rby[INDEX[s], 0]
            full = jnp.where(row8 == 0, roll(rbxy[edge[(1, s)]], -X, 0), near)
            full = jnp.where(row8 == X + 1, roll(rbxy[edge[(-1, s)]], X, 0), full)
            beside = rby[INDEX[s], 1] + by[INDEX[-s], 0] + roll(full, 1, 0) + roll(full, -1, 0)
            for t in SIGNS:
                beside = beside + rowshift(near, t, rbyzr[edge[(s, t)]], lane8)
            CY[s] = chemical(near, beside)

            near = rbz[INDEX[s]]
            full = jnp.where(lane == 0, roll(rbxz[edge[(1, s)]], -X, 1), near)
            full = jnp.where(lane == X + 1, roll(rbxz[edge[(-1, s)]], X, 1), full)
            beside = roll(near, -LANES, 1) + bz[INDEX[-s]] + roll(full, 1, 1) + roll(full, -1, 1)
            for t in SIGNS:
                k = 7 if t == 1 else 0
                beside = beside + yshift(near, t, rbyzc[edge[(t, s)], k : k + 1, :])
            CZ[s] = chemical(near, beside)

        diffused = []
        for x in range(X):
            c = C[x]
            cy_up = yshift(c, -1, CY[-1][1 + x : 2 + x, :])
            cy_dn = yshift(c, 1, CY[1][1 + x : 2 + x, :])
            cz_up = zshift(c, -1, CZ[-1], 1 + x)
            cz_dn = zshift(c, 1, CZ[1], 1 + x)
            diffused.append(
                C[x + 1] + C[x - 1] + cy_up + cy_dn + cz_up + cz_dn - 6.0 * c
            )
            scale = -0.5 * O[x]
            force = [scale * (C[x + 1] - C[x - 1]), scale * (cy_up - cy_dn), scale * (cz_up - cz_dn)]
            ps = [pops[i, x] for i in range(19)]
            rho, moms = moments(ps)
            inv = 1.0 / rho
            u = [m * inv for m in moms]
            v = [u[d] + force[d] * inv for d in range(3)]
            keep = 1.0 - 1.0 / relax_time
            mix = 1.0 / relax_time - 1.0
            usq = u[0] * u[0] + u[1] * u[1] + u[2] * u[2]
            vsq = v[0] * v[0] + v[1] * v[1] + v[2] * v[2]
            flat = rho * ((mix + 1.0) - 1.5 * (mix * usq + vsq))
            out = [None] * 19
            out[0] = keep * ps[0] + WEIGHTS[0] * flat
            for i in range(1, 19, 2):
                a, b = None, None
                for d in range(3):
                    if DIRS[i][d]:
                        tu = u[d] if DIRS[i][d] == 1 else -u[d]
                        tv = v[d] if DIRS[i][d] == 1 else -v[d]
                        a = tu if a is None else a + tu
                        b = tv if b is None else b + tv
                even = WEIGHTS[i] * flat + (4.5 * WEIGHTS[i]) * rho * (mix * a * a + b * b)
                odd = (3.0 * WEIGHTS[i]) * rho * (mix * a + b)
                out[i] = keep * ps[i] + even + odd
                out[i + 1] = keep * ps[i + 1] + even - odd
            for i in range(19):
                post[i, x] = out[i]
            for s in SIGNS:
                if x == (X - 1 if s == 1 else 0):
                    for slot, i in enumerate(CROSS[0][s]):
                        ax[INDEX[s], slot] = out[i]
                y = Y - 1 if s == 1 else 0
                for slot, i in enumerate(CROSS[1][s]):
                    ay[INDEX[s], slot, 1 + x : 2 + x, :] = out[i][y : y + 1, :]
        for s in SIGNS:
            az[INDEX[s]] = pack(
                [[(post[i, x], Z - 1 if s == 1 else 0) for x in range(X)] for i in CROSS[2][s]], s
            )

        messages = []
        for s in SIGNS:
            si = INDEX[s]
            messages.append((ax.at[si], rax.at[si], (s, 0, 0)))
            messages.append((ay.at[si], ray.at[si], (0, s, 0)))
            messages.append((az.at[si], raz.at[si], (0, 0, s)))
        for e, (a, b) in enumerate(EDGES):
            slot = CROSS[1][b].index(DIRS.index((a, b, 0)))
            messages.append((ay.at[INDEX[b], slot], raxy.at[e], (a, b, 0)))
            messages.append((az.at[INDEX[b]], raxz.at[e], (a, 0, b)))
            slot = CROSS[1][a].index(DIRS.index((0, a, b)))
            messages.append((ay.at[INDEX[a], slot], rayz.at[e], (0, a, b)))
        finish(run(messages, sa, ra))

        flows = []
        for x in range(X):
            ps = []
            for i, (cx, cy, cz) in enumerate(DIRS):
                xs = x - cx
                own = 0 <= xs < X
                far = X - 1 if cx == 1 else 0
                p = post[i, xs] if own else rax[INDEX[cx], CROSS[0][cx].index(i)]
                if cz:
                    at = CROSS[2][cz].index(i) * LANES + 1
                    if own:
                        p = zshift(p, cz, raz[INDEX[cz]], at + xs)
                    else:
                        p = zshift(p, cz, raxz[edge[(cx, cz)]], at + far)
                if cy:
                    if own:
                        halo = ray[INDEX[cy], CROSS[1][cy].index(i), 1 + xs : 2 + xs, :]
                    else:
                        halo = raxy[edge[(cx, cy)], 1 + far : 2 + far, :]
                    if cz:
                        halo = rowshift(halo, cz, rayz[edge[(cy, cz)], 1 + x : 2 + x, :], lane1)
                    p = yshift(p, cy, halo)
                pops[i, x] = p
                ps.append(p)
            rho, moms = moments(ps)
            inv = 1.0 / rho
            flows.append([m * inv for m in moms])

        for s in SIGNS:
            si = INDEX[s]
            y = Y - 1 if s == 1 else 0
            cx_[si] = flows[X - 1 if s == 1 else 0][0]
            for x in range(X):
                cy_[si, 1 + x : 2 + x, :] = flows[x][1][y : y + 1, :]
            cz_[si] = pack([[(flows[x][2], Z - 1 if s == 1 else 0) for x in range(X)]], s)
        messages = []
        for s in SIGNS:
            si = INDEX[s]
            messages.append((cx_.at[si], rcx.at[si], (s, 0, 0)))
            messages.append((cy_.at[si], rcy.at[si], (0, s, 0)))
            messages.append((cz_.at[si], rcz.at[si], (0, 0, s)))
        finish(run(messages, sc, rc))

        for x in range(X):
            f, pair = flows[x], pairs[x]
            fx_up = flows[x + 1][0] if x + 1 < X else rcx[1]
            fx_dn = flows[x - 1][0] if x > 0 else rcx[0]
            change = (f[0] + fx_up) * pair[(0, -1)] - (f[0] + fx_dn) * pair[(0, 1)]
            for s in SIGNS:
                fy = yshift(f[1], s, rcy[INDEX[s], 1 + x : 2 + x, :])
                fz = zshift(f[2], s, rcz[INDEX[s]], 1 + x)
                part = (f[1] + fy) * pair[(1, s)] + (f[2] + fz) * pair[(2, s)]
                change = change - part if s == 1 else change + part
            order[x] = O[x] - (0.25 * change - mobility * diffused[x])
        return carry

    lax.fori_loop(0, ITERS, step, 0)


def on_device(sizes, order_param, density, velocity):
    X, Y, Z = order_param.shape
    f32 = jnp.float32
    plane, rows = (Y, Z), (8, Z)
    vmem = [
        (19, X, Y, Z),
        (2, 5) + plane, (2, 5) + rows, (2,) + plane,
        (2, 5) + plane, (2, 5) + rows, (2,) + plane,
        (4,) + rows, (4,) + plane, (4,) + rows,
        (2, 2) + rows, (2,) + plane,
        (2, 2) + plane, (2, 2) + rows, (2,) + plane,
        (4,) + rows, (4,) + plane, (4,) + rows, (4,) + rows,
        (2,) + plane, (2,) + rows, (2,) + plane,
        (2,) + plane, (2,) + rows, (2,) + plane,
    ]
    sems = [18, 18, 22, 22, 6, 6]
    spec = pl.BlockSpec(memory_space=pltpu.VMEM)
    return pl.pallas_call(
        functools.partial(kernel, sizes),
        out_shape=(
            jax.ShapeDtypeStruct((X, Y, Z), f32),
            jax.ShapeDtypeStruct((19, X, Y, Z), f32),
        ),
        in_specs=[spec] * 3,
        out_specs=(spec, spec),
        scratch_shapes=[pltpu.VMEM(s, f32) for s in vmem]
        + [pltpu.SemaphoreType.DMA((n,)) for n in sems],
        compiler_params=pltpu.CompilerParams(collective_id=0, has_side_effects=True),
    )(order_param, density, velocity)


def solution(mesh):
    sizes = tuple(mesh.shape[a] for a in ("gx", "gy", "gz"))
    return jax.shard_map(
        functools.partial(on_device, sizes),
        mesh=mesh,
        in_specs=(P("gx", "gy", "gz"), P("gx", "gy", "gz"), P(None, "gx", "gy", "gz")),
        out_specs=(P("gx", "gy", "gz"), P(None, "gx", "gy", "gz")),
        check_vma=False,
    )
```

profile of v0, /device:TPU:0, one launch (start us, length us, event | category | flops | bytes accessed | tf_op | source)
XLA Modules:
  0.0 81.9 jit_solution(7709039325209929729)
XLA Ops:
  0.6 77.9 %shard_map.50 = (f32[4,16,128]{2,1,0:T(8,128)}, f32[19,4,16,128]{3,2,1,0:T(8,128)}) custom-call(f32[4,16,128]{2,1,0:T(8,128)} %order_in.1, f32[4,16,128]{2,1,0:T(8,128)} %dens_in.1, f32[3,4,16,128]{3,2,1,0:T(8,128)} %vel_in.1), custom_call_target="tpu_custom_call" | custom-call | tf_op jit(solution)/shard_map/pallas_call | solution.py:383
  78.6 1.4 %copy.7 = f32[4,16,128]{2,1,0:T(8,128)} copy(f32[4,16,128]{2,1,0:T(8,128)} %get-tuple-element.4) | data formatting | bytes 65536
  79.9 2.0 %copy.8 = f32[19,4,16,128]{3,2,1,0:T(8,128)} copy(f32[19,4,16,128]{3,2,1,0:T(8,128)} %get-tuple-element.5) | data formatting | bytes 1245184
where the time goes:
time: 82.2 us; the launch traced here: 81.9 us
  Pallas kernels  77.9 us (95%)
  local copies, waits for them, and re-layouts  3.33 us (4%)
    pallas_call x1, Pallas kernels, on_device(): pl.pallas_call(functools.partial(kernel, sizes), out_shape=(jax.ShapeDtyp...  77.9 us
    unnamed x2, local copies, waits for them, and re-layouts  3.33 us

commit v1 on v0

--- a/solution.py
+++ b/solution.py
@@ -56,10 +56,10 @@
 
 
 def kernel(sizes, order_in, dens_in, vel_in, order, pops, post, *scratch):
-    (ax, ay, az, rax, ray, raz, raxy, raxz, rayz) = scratch[0:9]
-    (by, bz, rbx, rby, rbz, rbxy, rbxz, rbyzr, rbyzc) = scratch[9:18]
-    (cx_, cy_, cz_, rcx, rcy, rcz) = scratch[18:24]
-    (sa, ra, sb, rb, sc, rc) = scratch[24:30]
+    (ax, ay, az, rax, ray, raz, ae, rae) = scratch[0:8]
+    (by, bz, rbx, rby, rbz, be, rbe) = scratch[8:15]
+    (cx_, cy_, cz_, rcx, rcy, rcz) = scratch[15:21]
+    (sa, ra, sb, rb, sc, rc) = scratch[21:27]
     X, Y, Z = order.shape
     me = [lax.axis_index(a) for a in ("gx", "gy", "gz")]
 
@@ -96,8 +96,32 @@
     def yshift(v, s, halo):
         return jnp.where(row == yend(s), jnp.broadcast_to(halo, v.shape), roll(v, s, 0))
 
-    def rowshift(v, s, edge, lanes):
-        return jnp.where(lanes == zend(s), roll(edge, s, 1), roll(v, s, 1))
+    def zinsert(v, s, col, lanes):
+        return jnp.where(lanes == zend(s), jnp.broadcast_to(col, v.shape), roll(v, s, 1))
+
+    def to_row(v, z):
+        col = jnp.broadcast_to(v[:, z : z + 1], v.shape)
+        return jnp.sum(jnp.where(lane == row, col, 0.0), axis=0, keepdims=True)
+
+    def to_col(v, lanes, rows):
+        v = jnp.broadcast_to(v, lanes.shape)
+        return jnp.sum(jnp.where(lanes == rows, v, 0.0), axis=1, keepdims=True)
+
+    def xsrc(s):
+        return X - 1 if s == 1 else 0
+
+    def ysrc(s):
+        return Y - 1 if s == 1 else 0
+
+    def zsrc(s):
+        return Z - 1 if s == 1 else 0
+
+    def corners(planes, b, c):
+        y, acc = ysrc(b), jnp.zeros((1, Z), jnp.float32)
+        for x in range(X):
+            cells = roll(planes[x][y : y + 1, :], 1 + x - zsrc(c), 1)
+            acc = jnp.where(lane1 == 1 + x, cells, acc)
+        return acc
 
     def pack(fields, s):
         acc = jnp.zeros((Y, Z), jnp.float32)
@@ -186,12 +210,41 @@
             messages.append((by.at[si], rby.at[si], (0, s, 0)))
             messages.append((bz.at[si], rbz.at[si], (0, 0, s)))
         for e, (a, b) in enumerate(EDGES):
-            messages.append((by.at[INDEX[b], 0], rbxy.at[e], (a, b, 0)))
-            messages.append((bz.at[INDEX[b]], rbxz.at[e], (a, 0, b)))
-            messages.append((by.at[INDEX[a], 0], rbyzr.at[e], (0, a, b)))
-            half = bz.at[INDEX[b], pl.ds(Y - 8, 8)] if a == 1 else bz.at[INDEX[b], pl.ds(0, 8)]
-            messages.append((half, rbyzc.at[e], (0, a, b)))
-        finish(run(messages, sb, rb))
+            be[e] = O[xsrc(a)][ysrc(b) : ysrc(b) + 1, :]
+            be[4 + e] = to_row(O[xsrc(a)], zsrc(b))
+            be[8 + e] = corners(O, a, b)
+            messages.append((be.at[e], rbe.at[e], (a, b, 0)))
+            messages.append((be.at[4 + e], rbe.at[4 + e], (a, 0, b)))
+            messages.append((be.at[8 + e], rbe.at[8 + e], (0, a, b)))
+        flying = run(messages, sb, rb)
+
+        keep = 1.0 - 1.0 / relax_time
+        mix = 1.0 / relax_time - 1.0
+
+        def along(i, w):
+            a = None
+            for d in range(3):
+                if DIRS[i][d]:
+                    t = w[d] if DIRS[i][d] == 1 else -w[d]
+                    a = t if a is None else a + t
+            return a
+
+        moved = []
+        for x in range(X):
+            ps = [pops[i, x] for i in range(19)]
+            rho, moms = moments(ps)
+            inv = 1.0 / rho
+            u = [m * inv for m in moms]
+            flat = (mix * rho) * (1.0 - 1.5 * (u[0] * u[0] + u[1] * u[1] + u[2] * u[2]))
+            post[0, x] = keep * ps[0] + WEIGHTS[0] * flat
+            for i in range(1, 19, 2):
+                a = along(i, u)
+                even = WEIGHTS[i] * flat + (4.5 * mix * WEIGHTS[i]) * rho * (a * a)
+                odd = (3.0 * mix * WEIGHTS[i]) * rho * a
+                post[i, x] = keep * ps[i] + even + odd
+                post[i + 1, x] = keep * ps[i + 1] + even - odd
+            moved.append((rho, inv, u))
+        finish(flying)
 
         edge = {ab: e for e, ab in enumerate(EDGES)}
         OX = {-2: rbx[0, 0], -1: rbx[0, 1], X: rbx[1, 0], X + 1: rbx[1, 1]}
@@ -213,31 +266,33 @@
             pairs.append({k: O[x] + v for k, v in near.items()})
         for s in SIGNS:
             x = -1 if s == 1 else X
-            far = X - 1 if s == 1 else 0
             p = OX[x]
             beside = OX[x - 1] + OX[x + 1]
             for t in SIGNS:
                 e = edge[(s, t)]
-                beside = beside + yshift(p, t, rbxy[e, 1 + far : 2 + far, :])
-                beside = beside + zshift(p, t, rbxz[e], 1 + far)
+                beside = beside + yshift(p, t, rbe[e])
+                beside = beside + zinsert(p, t, to_col(rbe[4 + e], lane, row), lane)
             C[x] = chemical(p, beside)
         CY, CZ = {}, {}
         for s in SIGNS:
             near = rby[INDEX[s], 0]
-            full = jnp.where(row8 == 0, roll(rbxy[edge[(1, s)]], -X, 0), near)
-            full = jnp.where(row8 == X + 1, roll(rbxy[edge[(-1, s)]], X, 0), full)
+            full = jnp.where(row8 == 0, jnp.broadcast_to(rbe[edge[(1, s)]], near.shape), near)
+            after = jnp.broadcast_to(rbe[edge[(-1, s)]], near.shape)
+            full = jnp.where(row8 == X + 1, after, full)
             beside = rby[INDEX[s], 1] + by[INDEX[-s], 0] + roll(full, 1, 0) + roll(full, -1, 0)
             for t in SIGNS:
-                beside = beside + rowshift(near, t, rbyzr[edge[(s, t)]], lane8)
+                col = to_col(rbe[8 + edge[(s, t)]], lane8, row8)
+                beside = beside + zinsert(near, t, col, lane8)
             CY[s] = chemical(near, beside)
 
             near = rbz[INDEX[s]]
-            full = jnp.where(lane == 0, roll(rbxz[edge[(1, s)]], -X, 1), near)
-            full = jnp.where(lane == X + 1, roll(rbxz[edge[(-1, s)]], X, 1), full)
+            before = jnp.broadcast_to(to_col(rbe[4 + edge[(1, s)]], lane, row), near.shape)
+            after = jnp.broadcast_to(to_col(rbe[4 + edge[(-1, s)]], lane, row), near.shape)
+            full = jnp.where(lane == 0, before, near)
+            full = jnp.where(lane == X + 1, after, full)
             beside = roll(near, -LANES, 1) + bz[INDEX[-s]] + roll(full, 1, 1) + roll(full, -1, 1)
             for t in SIGNS:
-                k = 7 if t == 1 else 0
-                beside = beside + yshift(near, t, rbyzc[edge[(t, s)], k : k + 1, :])
+                beside = beside + yshift(near, t, rbe[8 + edge[(t, s)]])
             CZ[s] = chemical(near, beside)
 
         diffused = []
@@ -252,30 +307,17 @@
             )
             scale = -0.5 * O[x]
             force = [scale * (C[x + 1] - C[x - 1]), scale * (cy_up - cy_dn), scale * (cz_up - cz_dn)]
-            ps = [pops[i, x] for i in range(19)]
-            rho, moms = moments(ps)
-            inv = 1.0 / rho
-            u = [m * inv for m in moms]
+            rho, inv, u = moved[x]
             v = [u[d] + force[d] * inv for d in range(3)]
-            keep = 1.0 - 1.0 / relax_time
-            mix = 1.0 / relax_time - 1.0
-            usq = u[0] * u[0] + u[1] * u[1] + u[2] * u[2]
-            vsq = v[0] * v[0] + v[1] * v[1] + v[2] * v[2]
-            flat = rho * ((mix + 1.0) - 1.5 * (mix * usq + vsq))
+            flat = rho * (1.0 - 1.5 * (v[0] * v[0] + v[1] * v[1] + v[2] * v[2]))
             out = [None] * 19
-            out[0] = keep * ps[0] + WEIGHTS[0] * flat
+            out[0] = post[0, x] + WEIGHTS[0] * flat
             for i in range(1, 19, 2):
-                a, b = None, None
-                for d in range(3):
-                    if DIRS[i][d]:
-                        tu = u[d] if DIRS[i][d] == 1 else -u[d]
-                        tv = v[d] if DIRS[i][d] == 1 else -v[d]
-                        a = tu if a is None else a + tu
-                        b = tv if b is None else b + tv
-                even = WEIGHTS[i] * flat + (4.5 * WEIGHTS[i]) * rho * (mix * a * a + b * b)
-                odd = (3.0 * WEIGHTS[i]) * rho * (mix * a + b)
-                out[i] = keep * ps[i] + even + odd
-                out[i + 1] = keep * ps[i + 1] + even - odd
+                a = along(i, v)
+                even = WEIGHTS[i] * flat + (4.5 * WEIGHTS[i]) * rho * (a * a)
+                odd = (3.0 * WEIGHTS[i]) * rho * a
+                out[i] = post[i, x] + even + odd
+                out[i + 1] = post[i + 1, x] + even - odd
             for i in range(19):
                 post[i, x] = out[i]
             for s in SIGNS:
@@ -297,11 +339,13 @@
             messages.append((ay.at[si], ray.at[si], (0, s, 0)))
             messages.append((az.at[si], raz.at[si], (0, 0, s)))
         for e, (a, b) in enumerate(EDGES):
-            slot = CROSS[1][b].index(DIRS.index((a, b, 0)))
-            messages.append((ay.at[INDEX[b], slot], raxy.at[e], (a, b, 0)))
-            messages.append((az.at[INDEX[b]], raxz.at[e], (a, 0, b)))
-            slot = CROSS[1][a].index(DIRS.index((0, a, b)))
-            messages.append((ay.at[INDEX[a], slot], rayz.at[e], (0, a, b)))
+            ae[e] = post[DIRS.index((a, b, 0)), xsrc(a)][ysrc(b) : ysrc(b) + 1, :]
+            ae[4 + e] = to_row(post[DIRS.index((a, 0, b)), xsrc(a)], zsrc(b))
+            i = DIRS.index((0, a, b))
+            ae[8 + e] = corners([post[i, x] for x in range(X)], a, b)
+            messages.append((ae.at[e], rae.at[e], (a, b, 0)))
+            messages.append((ae.at[4 + e], rae.at[4 + e], (a, 0, b)))
+            messages.append((ae.at[8 + e], rae.at[8 + e], (0, a, b)))
         finish(run(messages, sa, ra))
 
         flows = []
@@ -310,21 +354,21 @@
             for i, (cx, cy, cz) in enumerate(DIRS):
                 xs = x - cx
                 own = 0 <= xs < X
-                far = X - 1 if cx == 1 else 0
                 p = post[i, xs] if own else rax[INDEX[cx], CROSS[0][cx].index(i)]
                 if cz:
                     at = CROSS[2][cz].index(i) * LANES + 1
                     if own:
                         p = zshift(p, cz, raz[INDEX[cz]], at + xs)
                     else:
-                        p = zshift(p, cz, raxz[edge[(cx, cz)]], at + far)
+                        p = zinsert(p, cz, to_col(rae[4 + edge[(cx, cz)]], lane, row), lane)
                 if cy:
                     if own:
                         halo = ray[INDEX[cy], CROSS[1][cy].index(i), 1 + xs : 2 + xs, :]
                     else:
-                        halo = raxy[edge[(cx, cy)], 1 + far : 2 + far, :]
+                        halo = rae[edge[(cx, cy)]]
                     if cz:
-                        halo = rowshift(halo, cz, rayz[edge[(cy, cz)], 1 + x : 2 + x, :], lane1)
+                        cell = roll(rae[8 + edge[(cy, cz)]], zend(cz) - (1 + x), 1)
+                        halo = jnp.where(lane1 == zend(cz), cell, roll(halo, cz, 1))
                     p = yshift(p, cy, halo)
                 pops[i, x] = p
                 ps.append(p)
@@ -371,14 +415,14 @@
         (19, X, Y, Z),
         (2, 5) + plane, (2, 5) + rows, (2,) + plane,
         (2, 5) + plane, (2, 5) + rows, (2,) + plane,
-        (4,) + rows, (4,) + plane, (4,) + rows,
+        (12, 1, Z), (12, 1, Z),
         (2, 2) + rows, (2,) + plane,
         (2, 2) + plane, (2, 2) + rows, (2,) + plane,
-        (4,) + rows, (4,) + plane, (4,) + rows, (4,) + rows,
+        (12, 1, Z), (12, 1, Z),
         (2,) + plane, (2,) + rows, (2,) + plane,
         (2,) + plane, (2,) + rows, (2,) + plane,
     ]
-    sems = [18, 18, 22, 22, 6, 6]
+    sems = [18, 18, 18, 18, 6, 6]
     spec = pl.BlockSpec(memory_space=pltpu.VMEM)
     return pl.pallas_call(
         functools.partial(kernel, sizes),

time: 82.2 us -> 79.2 us (0.964)
  Pallas kernels: 77.9 us -> 75 us
    pallas_call x1, Pallas kernels: 77.9 us -> 75 us  [on_device(): pl.pallas_call(functools.partial(kernel, sizes), out_shape=(jax.ShapeDtyp...]
where the time goes in v1:
time: 79.2 us; the launch traced here: 78.9 us
  Pallas kernels  75 us (95%)
  local copies, waits for them, and re-layouts  3.33 us (4%)
    pallas_call x1, Pallas kernels, on_device(): pl.pallas_call(functools.partial(kernel, sizes), out_shape=(jax.ShapeDtyp...  75 us
    unnamed x2, local copies, waits for them, and re-layouts  3.33 us

profile of v1, /device:TPU:0, one launch (start us, length us, event | category | flops | bytes accessed | tf_op | source)
XLA Modules:
  0.0 78.9 jit_solution(1207101864735886821)
XLA Ops:
  0.6 75.0 %shard_map.50 = (f32[4,16,128]{2,1,0:T(8,128)}, f32[19,4,16,128]{3,2,1,0:T(8,128)}) custom-call(f32[4,16,128]{2,1,0:T(8,128)} %order_in.1, f32[4,16,128]{2,1,0:T(8,128)} %dens_in.1, f32[3,4,16,128]{3,2,1,0:T(8,128)} %vel_in.1), custom_call_target="tpu_custom_call" | custom-call | tf_op jit(solution)/shard_map/pallas_call | solution.py:427
  75.6 1.4 %copy.7 = f32[4,16,128]{2,1,0:T(8,128)} copy(f32[4,16,128]{2,1,0:T(8,128)} %get-tuple-element.4) | data formatting | bytes 65536
  77.0 2.0 %copy.8 = f32[19,4,16,128]{3,2,1,0:T(8,128)} copy(f32[19,4,16,128]{3,2,1,0:T(8,128)} %get-tuple-element.5) | data formatting | bytes 1245184

commit v2 on v1

--- a/solution.py
+++ b/solution.py
@@ -132,9 +132,10 @@
                 acc = jnp.where(lane == at, roll(planes[x][0], at - depth_lane, 1), acc)
         return acc
 
-    def run(messages, ssem, rsem):
+    def run(messages, ssem, rsem, first=0):
         copies = []
-        for k, (src, dst, off) in enumerate(messages):
+        messages = sorted(messages, key=lambda m: (m[2][1] == 0, -sum(map(abs, m[2]))))
+        for k, (src, dst, off) in enumerate(messages, first):
             copy = pltpu.make_async_remote_copy(
                 src_ref=src,
                 dst_ref=dst,
@@ -173,6 +174,8 @@
                 pops[i, x] = WEIGHTS[i] * r * (usq + 3.0 * along + 4.5 * along * along)
     pl.semaphore_wait(barrier, len(neighbours()))
 
+    outer_first = sorted(range(X), key=lambda x: (min(x, X - 1 - x), x))
+
     def moments(ps):
         rho = ps[0]
         for i in range(1, 19):
@@ -195,20 +198,12 @@
                 y = Y - 1 - depth if s == 1 else depth
                 for x in range(X):
                     by[si, depth, 1 + x : 2 + x, :] = O[x][y : y + 1, :]
-            bz[si] = pack(
-                [
-                    [(O[x], Z - 1 - depth if s == 1 else depth) for x in range(X)]
-                    for depth in range(2)
-                ],
-                s,
-            )
         messages = []
         for s in SIGNS:
             si = INDEX[s]
             planes = order.at[pl.ds(X - 2, 2)] if s == 1 else order.at[pl.ds(0, 2)]
             messages.append((planes, rbx.at[si], (s, 0, 0)))
             messages.append((by.at[si], rby.at[si], (0, s, 0)))
-            messages.append((bz.at[si], rbz.at[si], (0, 0, s)))
         for e, (a, b) in enumerate(EDGES):
             be[e] = O[xsrc(a)][ysrc(b) : ysrc(b) + 1, :]
             be[4 + e] = to_row(O[xsrc(a)], zsrc(b))
@@ -217,6 +212,18 @@
             messages.append((be.at[4 + e], rbe.at[4 + e], (a, 0, b)))
             messages.append((be.at[8 + e], rbe.at[8 + e], (0, a, b)))
         flying = run(messages, sb, rb)
+        messages = []
+        for s in SIGNS:
+            si = INDEX[s]
+            bz[si] = pack(
+                [
+                    [(O[x], Z - 1 - depth if s == 1 else depth) for x in range(X)]
+                    for depth in range(2)
+                ],
+                s,
+            )
+            messages.append((bz.at[si], rbz.at[si], (0, 0, s)))
+        flying = flying + run(messages, sb, rb, len(flying))
 
         keep = 1.0 - 1.0 / relax_time
         mix = 1.0 / relax_time - 1.0
@@ -295,16 +302,15 @@
                 beside = beside + yshift(near, t, rbe[8 + edge[(t, s)]])
             CZ[s] = chemical(near, beside)
 
-        diffused = []
-        for x in range(X):
+        diffused = {}
+        flying = []
+        for place, x in enumerate(outer_first):
             c = C[x]
             cy_up = yshift(c, -1, CY[-1][1 + x : 2 + x, :])
             cy_dn = yshift(c, 1, CY[1][1 + x : 2 + x, :])
             cz_up = zshift(c, -1, CZ[-1], 1 + x)
             cz_dn = zshift(c, 1, CZ[1], 1 + x)
-            diffused.append(
-                C[x + 1] + C[x - 1] + cy_up + cy_dn + cz_up + cz_dn - 6.0 * c
-            )
+            diffused[x] = C[x + 1] + C[x - 1] + cy_up + cy_dn + cz_up + cz_dn - 6.0 * c
             scale = -0.5 * O[x]
             force = [scale * (C[x + 1] - C[x - 1]), scale * (cy_up - cy_dn), scale * (cz_up - cz_dn)]
             rho, inv, u = moved[x]
@@ -327,29 +333,37 @@
                 y = Y - 1 if s == 1 else 0
                 for slot, i in enumerate(CROSS[1][s]):
                     ay[INDEX[s], slot, 1 + x : 2 + x, :] = out[i][y : y + 1, :]
+            if place == 1:
+                early = []
+                for s in SIGNS:
+                    early.append((ax.at[INDEX[s]], rax.at[INDEX[s]], (s, 0, 0)))
+                for e, (a, b) in enumerate(EDGES):
+                    ae[e] = post[DIRS.index((a, b, 0)), xsrc(a)][ysrc(b) : ysrc(b) + 1, :]
+                    ae[4 + e] = to_row(post[DIRS.index((a, 0, b)), xsrc(a)], zsrc(b))
+                    early.append((ae.at[e], rae.at[e], (a, b, 0)))
+                    early.append((ae.at[4 + e], rae.at[4 + e], (a, 0, b)))
+                flying = run(early, sa, ra)
+
+        messages = []
+        for e, (a, b) in enumerate(EDGES):
+            i = DIRS.index((0, a, b))
+            ae[8 + e] = corners([post[i, x] for x in range(X)], a, b)
+            messages.append((ae.at[8 + e], rae.at[8 + e], (0, a, b)))
+        for s in SIGNS:
+            messages.append((ay.at[INDEX[s]], ray.at[INDEX[s]], (0, s, 0)))
+        flying = flying + run(messages, sa, ra, len(flying))
+        messages = []
         for s in SIGNS:
             az[INDEX[s]] = pack(
                 [[(post[i, x], Z - 1 if s == 1 else 0) for x in range(X)] for i in CROSS[2][s]], s
             )
-
-        messages = []
-        for s in SIGNS:
-            si = INDEX[s]
-            messages.append((ax.at[si], rax.at[si], (s, 0, 0)))
-            messages.append((ay.at[si], ray.at[si], (0, s, 0)))
-            messages.append((az.at[si], raz.at[si], (0, 0, s)))
-        for e, (a, b) in enumerate(EDGES):
-            ae[e] = post[DIRS.index((a, b, 0)), xsrc(a)][ysrc(b) : ysrc(b) + 1, :]
-            ae[4 + e] = to_row(post[DIRS.index((a, 0, b)), xsrc(a)], zsrc(b))
-            i = DIRS.index((0, a, b))
-            ae[8 + e] = corners([post[i, x] for x in range(X)], a, b)
-            messages.append((ae.at[e], rae.at[e], (a, b, 0)))
-            messages.append((ae.at[4 + e], rae.at[4 + e], (a, 0, b)))
-            messages.append((ae.at[8 + e], rae.at[8 + e], (0, a, b)))
-        finish(run(messages, sa, ra))
-
-        flows = []
-        for x in range(X):
+            messages.append((az.at[INDEX[s]], raz.at[INDEX[s]], (0, 0, s)))
+        flying = flying + run(messages, sa, ra, len(flying))
+        finish(flying)
+
+        flows = {}
+        flying = []
+        for place, x in enumerate(outer_first):
             ps = []
             for i, (cx, cy, cz) in enumerate(DIRS):
                 xs = x - cx
@@ -374,22 +388,26 @@
                 ps.append(p)
             rho, moms = moments(ps)
             inv = 1.0 / rho
-            flows.append([m * inv for m in moms])
+            flows[x] = [m * inv for m in moms]
+            if place == 1:
+                early = []
+                for s in SIGNS:
+                    cx_[INDEX[s]] = flows[xsrc(s)][0]
+                    early.append((cx_.at[INDEX[s]], rcx.at[INDEX[s]], (s, 0, 0)))
+                flying = run(early, sc, rc)
 
         for s in SIGNS:
             si = INDEX[s]
             y = Y - 1 if s == 1 else 0
-            cx_[si] = flows[X - 1 if s == 1 else 0][0]
             for x in range(X):
                 cy_[si, 1 + x : 2 + x, :] = flows[x][1][y : y + 1, :]
             cz_[si] = pack([[(flows[x][2], Z - 1 if s == 1 else 0) for x in range(X)]], s)
         messages = []
         for s in SIGNS:
             si = INDEX[s]
-            messages.append((cx_.at[si], rcx.at[si], (s, 0, 0)))
             messages.append((cy_.at[si], rcy.at[si], (0, s, 0)))
             messages.append((cz_.at[si], rcz.at[si], (0, 0, s)))
-        finish(run(messages, sc, rc))
+        finish(flying + run(messages, sc, rc, len(flying)))
 
         for x in range(X):
             f, pair = flows[x], pairs[x]

time: 79.2 us -> 76.5 us (0.966)
  Pallas kernels: 75 us -> 72.3 us
    pallas_call x1, Pallas kernels: 75 us -> 72.3 us  [on_device(): pl.pallas_call(functools.partial(kernel, sizes), out_shape=(jax.ShapeDtyp...]
where the time goes in v2:
time: 76.5 us; the launch traced here: 76.3 us
  Pallas kernels  72.3 us (95%)
  local copies, waits for them, and re-layouts  3.33 us (4%)
    pallas_call x1, Pallas kernels, on_device(): pl.pallas_call(functools.partial(kernel, sizes), out_shape=(jax.ShapeDtyp...  72.3 us
    unnamed x2, local copies, waits for them, and re-layouts  3.33 us

profile of v2, /device:TPU:0, one launch (start us, length us, event | category | flops | bytes accessed | tf_op | source)
XLA Modules:
  0.0 76.3 jit_solution(1822268335991525031)
XLA Ops:
  0.6 72.3 %shard_map.50 = (f32[4,16,128]{2,1,0:T(8,128)}, f32[19,4,16,128]{3,2,1,0:T(8,128)}) custom-call(f32[4,16,128]{2,1,0:T(8,128)} %order_in.1, f32[4,16,128]{2,1,0:T(8,128)} %dens_in.1, f32[3,4,16,128]{3,2,1,0:T(8,128)} %vel_in.1), custom_call_target="tpu_custom_call" | custom-call | tf_op jit(solution)/shard_map/pallas_call | solution.py:445
  72.9 1.4 %copy.7 = f32[4,16,128]{2,1,0:T(8,128)} copy(f32[4,16,128]{2,1,0:T(8,128)} %get-tuple-element.4) | data formatting | bytes 65536
  74.3 2.0 %copy.8 = f32[19,4,16,128]{3,2,1,0:T(8,128)} copy(f32[19,4,16,128]{3,2,1,0:T(8,128)} %get-tuple-element.5) | data formatting | bytes 1245184
